TPU v7x, 32 devices: a 4x4x1 block of a 4x4x8 slice. The times are simulated.
32 devices in a mesh: batch: 1 (over z), col: 4 (over y), row: 8 (over x, core).
Axes of the slice: x: 4, y: 4, z: 1, core: 2. Of those that a mesh axis runs over, the one named last changes fastest.
The devices are a block of a 4x4x8 slice.
Arguments:
- lower_cyc: float32 [2048, 2048], P(('batch', 'row'), 'col')
Outputs:
- output: float32 [2048, 2048], P(('batch', 'row'), 'col')
All inputs are finite; a program needn't handle non-finite values.
Results may differ from a plain program's by a relative error of at most 0.001.
Values sent between devices are 32-bit elements.
A program may use at most 768 MiB of HBM per device.

v0:
```python
import functools

import jax
import jax.numpy as jnp
from jax import lax
from jax.experimental import pallas as pl
from jax.experimental.pallas import tpu as pltpu
from jax.sharding import PartitionSpec as P

BLK = 8
CORES = 2
LANES = 128
HALF = LANES // 2
WIDE = 2 * LANES
TALL = 4
GROUPS = 5
LEAVES = range(2)
PAIR = range(2)
SIDES = (-1, 1)
MESH = pl.DeviceIdType.MESH
F32 = jnp.float32


def dot(left, right):
    return jnp.dot(left, right, precision=lax.Precision.HIGHEST, preferred_element_type=F32)


def iota(shape, dim):
    return lax.broadcasted_iota(jnp.int32, shape, dim)


def halves(tiles, half):
    low = iota(tiles[0].shape, 1) < HALF
    out = []
    for first, second in ((tiles[0], tiles[1]), (tiles[2], tiles[3])):
        if half == 0:
            out.append(jnp.where(low, first, pltpu.roll(second, HALF, 1)))
        else:
            out.append(jnp.where(low, pltpu.roll(first, HALF, 1), second))
    return jnp.concatenate(out, axis=1)


class Net:
    def __init__(self, send, recv):
        self.send, self.recv, self.names = send, recv, {}

    def slot(self, side, name):
        held = [key for key in self.names if key[0] == side]
        return self.names.setdefault((side, name), len(held))

    def start(self, src, dst, device, send, recv):
        self.make(src, dst, device, send, recv).start()

    def make(self, src, dst, device, send, recv):
        return pltpu.make_async_remote_copy(
            src_ref=src, dst_ref=dst, send_sem=self.send.at[self.slot("send", send)], recv_sem=self.recv.at[self.slot("recv", recv)],
            device_id=device, device_id_type=MESH)

    def wait(self, name, like, side="recv"):
        sems = self.recv if side == "recv" else self.send
        pltpu.make_async_copy(like, like, sems.at[self.slot(side, name)]).wait()


def shift(val, lanes):
    return jnp.concatenate([pltpu.roll(val[:, LANES * i:LANES * (i + 1)], lanes % LANES, 1) for i in range(2)], axis=1)


def kernel(rows, cols, hbm_ref, o_ref, l_ref, U, G, C0, LF, PK, LI, WL, WR, ZM, ZS, TG, SX, YX, VV, SS, TP, load, send, recv):
    chips = rows // CORES
    row = lax.axis_index("row")
    y = lax.axis_index("col")
    x, core = row // CORES, row % CORES
    spot, hh = row % cols, row // cols
    net = Net(send, recv)
    first_half = core == 1

    def at(xx, cc, yy):
        return {"row": xx * CORES + cc, "col": yy}

    def xs(step):
        return lax.rem(x + step + chips, chips)

    def ys(step):
        return lax.rem(y + step + cols, cols)

    def along(axis, step, cc=core):
        return at(xs(step), cc, y) if axis == "x" else at(x, cc, ys(step))

    upper, lower, near, far = pl.ds(0, LANES), pl.ds(LANES, LANES), pl.ds(0, WIDE), pl.ds(WIDE, WIDE)
    windows = [(upper, near), (lower, far), (lower, near)]
    loads = [pltpu.make_async_copy(hbm_ref.at[w], l_ref.at[w], load.at[i]) for i, w in enumerate(windows)]
    for made in loads:
        made.start()
    partner = at(x, 1 - core, y)
    barrier = pltpu.get_barrier_semaphore()
    peers = [partner] + [along(axis, d, cc) for axis in "xy" for d in range(1, chips) for cc in range(CORES)]
    for peer in peers:
        pl.semaphore_signal(barrier, inc=1, device_id=peer, device_id_type=MESH)

    quarter = LANES // TALL
    for part in range(2):
        loads[part].wait()
        piece = l_ref[part * LANES:(part + 1) * LANES, part * WIDE:(part + 1) * WIDE]
        low = iota((quarter, LANES), 1) < HALF
        band = [piece[quarter * i:quarter * (i + 1)] for i in range(TALL)]
        packed = [jnp.where(low, band[2 * m][:, LANES * m:LANES * (m + 1)], band[2 * m + 1][:, LANES * m:LANES * (m + 1)])
                  for m in PAIR]
        packed.append(jnp.where(low, band[1][:, :LANES], pltpu.roll(band[3][:, LANES:], HALF, 1)))
        packed += [band[2][:, :LANES], band[3][:, :LANES]]
        tiles = [val.reshape(TALL, BLK, LANES) for val in packed]
        for g in range(GROUPS):
            U[part, g] = tiles[g]

        @pl.when(core == 1 - part)
        def _():
            for g in range(GROUPS):
                G[y, g, hh, spot] = tiles[g]

    loads[2].wait()
    C0[core, y] = l_ref[lower, near]
    pl.semaphore_wait(barrier, len(peers))

    axis_first = ["x", "y", "y"]

    def other(axis):
        return "y" if axis == "x" else "x"

    def source(g, f, s, k=None):
        xx, yy = (xs(f), ys(s)) if axis_first[g] == "x" else (xs(s), ys(f))
        return G.at[yy, g, xx // 2, pl.ds(2 * (xx % 2), 2) if k is None else 2 * (xx % 2) + k]

    def pass_on(g, f, s, k, step, name):
        piece = source(g, f, s, k)
        net.start(piece, piece, along(other(axis_first[g]), step), g, name)

    def pass_leaf(g, f):
        for s in SIDES:
            pass_on(g, f, 0, None, -s, (g, "far") if f == 2 else (g, f, s))
        if f == 2:
            pass_on(g, f, 0, None, 2, (g, "far"))

    def half_on(g, f, s):
        pass_on(g, f, s, 0 if s < 0 else 1, -s, (g, "far"))

    for axis in "xy":
        for step in SIDES:
            for part in range(2):
                net.start(U.at[part, pl.ds(0, 2)], G.at[y, pl.ds(0, 2), hh, spot], along(axis, step, 1 - part), "leaf", ("leaf", axis, -step))
    for g in LEAVES:
        for part in range(2):
            net.start(U.at[part, g], G.at[y, g, hh, spot], along(axis_first[g], 2, 1 - part), "leaf", (g, "two"))
    net.start(U.at[core], G.at[y, :, hh, spot], partner, "pair", "pair")
    for s in SIDES:
        net.start(l_ref.at[lower, near], C0.at[core, y], along("y", -s, 1), "c0", ("c0", s))

    @pl.when(core == 0)
    def _():
        net.start(l_ref.at[lower, near], C0.at[core, y], partner, "c0pair", "c0pair")


    def near_by(groups, name, count):
        for step in SIDES:
            for axis in "xy":
                net.wait((name, axis, step), G.at[0, pl.ds(0, count), 0, pl.ds(0, 2)])
                for g in groups:
                    if axis_first[g] == axis:
                        pass_leaf(g, step)
                    else:
                        half_on(g, 0, step)

    def two_away(groups):
        for g in groups:
            net.wait((g, "two"), G.at[0, 0, 0, pl.ds(0, 2)])
            pass_leaf(g, 2)

    def across(groups):
        for f in SIDES:
            for s in SIDES:
                for g in groups:
                    net.wait((g, f, s), source(g, f, s))
                    half_on(g, f, s)

    near_by(LEAVES, "leaf", 2)
    for part in range(2):
        for axis in "xy":
            for step in SIDES:
                net.start(U.at[part, 2], G.at[y, 2, hh, spot], along(axis, step, 1 - part), "link", ("link", axis, -step))
        net.start(U.at[part, 2], G.at[y, 2, hh, spot], along(axis_first[2], 2, 1 - part), "link", (2, "two"))
    two_away(LEAVES)
    across(LEAVES)
    net.wait("pair", U.at[0])
    near_by((2,), "link", 1)
    for d in range(1, chips):
        for part, axis in enumerate("yx"):
            net.start(U.at[part, pl.ds(3, 2)], G.at[y, pl.ds(3, 2), hh, spot], along(axis, d, 1 - part), "rest", "c1")


    @pl.when(first_half)
    def _():
        for s in SIDES:
            net.wait(("c0", s), C0.at[:, 0])
            piece = C0.at[0 if s < 0 else 1, ys(s)]
            net.start(piece, piece, along("y", -s), "c0far", "c0far")

    for g in LEAVES:
        net.wait((g, "far"), G.at[pl.ds(0, 3), g, 0])

    two_away((2,))
    lane = iota((BLK, LANES), 1)
    sub = iota((BLK, LANES), 0)
    block_of = (lane // BLK) % BLK
    diag = [[[None] * TALL for _ in range(TALL)] for _ in PAIR]
    inv = [[[None] * TALL for _ in range(TALL)] for _ in PAIR]
    for m in PAIR:
        for c in range(TALL):
            for k in range(c + 1):
                total = jnp.zeros((BLK, LANES), F32)
                for b in range(BLK):
                    total = jnp.where(block_of == b, G[k, m, b % 2, c, b // 2], total)
                diag[m][c][k] = total
                inv[m][c][k] = jnp.where(sub == lane % BLK, 1.0, 0.0) if c == k else jnp.zeros((BLK, LANES), F32)
    for t in range(BLK * TALL):
        ct, jt = t // BLK, t % BLK
        index = (lane // BLK) * BLK + jt
        for m in PAIR:
            spread = [jnp.take_along_axis(diag[m][c][ct], index, axis=1) for c in range(ct, TALL)]
            pivot = 1.0 / spread[0][jt:jt + 1, :]
            below = jnp.where(sub > jt, spread[0], 0.0)
            for k in range(ct + 1):
                solved = inv[m][ct][k][jt:jt + 1, :] * pivot
                inv[m][ct][k] = jnp.where(sub == jt, solved, inv[m][ct][k] - below * solved)
                for c in range(ct + 1, TALL):
                    inv[m][c][k] = inv[m][c][k] - spread[c - ct] * solved
    for m in PAIR:
        for c in range(TALL):
            tiles = [inv[m][c][k] if k <= c else jnp.zeros((BLK, LANES), F32) for k in range(TALL)]
            for e in PAIR:
                PK[2 * m + e, c] = halves(tiles, e)

    def gathered(k, g):
        return jnp.concatenate([G[k, g, b % 2, c, b // 2] for c in range(TALL) for b in range(BLK)], axis=0)

    for m in PAIR:
        tiles = [gathered(k, m) for k in range(cols)]
        for e in PAIR:
            LF[2 * m + e] = halves(tiles, e).reshape(TALL * BLK, BLK, WIDE)

    def double(m, nb):
        count, lanes = TALL * nb, BLK * nb
        size = BLK * count
        group = ((iota((BLK, WIDE), 1) % HALF) // BLK) // nb
        even = ((iota((size, WIDE), 1) % HALF) // BLK) // nb % 2 == 0

        def coupling(leaf):
            out = []
            for bb in range(nb):
                for c in range(TALL):
                    total = LF[leaf, c * BLK + nb + bb]
                    for s in range(3, BLK // nb, 2):
                        total = jnp.where(group == s - 1, LF[leaf, c * BLK + s * nb + bb], total)
                    out.append(total)
            return jnp.concatenate(out, axis=0)

        def spread(val, flip):
            tiles = val.reshape(count, BLK, WIDE)
            return jnp.concatenate([jnp.where(group == (b // nb) ^ flip, tiles[(b % nb) * TALL + c], 0.0)
                                    for c in range(TALL) for b in range(BLK)], axis=0)

        one, two = (PK[2 * m + e, 0:count].reshape(size, WIDE) for e in PAIR)
        temp = dot(jnp.where(even, coupling(2 * m), shift(coupling(2 * m + 1), lanes)),
                   spread(jnp.where(even, one, shift(two, lanes)), 0))
        corner = dot(jnp.where(even, shift(two, -lanes), one), spread(temp, 1))
        for e, (val, low) in enumerate(((one, corner), (two, shift(corner, -lanes)))):
            parts = (jnp.where(even, val, 0.0), jnp.where(even, -low, val))
            for half in PAIR:
                tiles = parts[half].reshape(count, BLK, WIDE)
                if nb < TALL:
                    PK[2 * m + e, half * count:(half + 1) * count] = tiles
                else:
                    for i in range(count):
                        LI[2 * m + e, (i % TALL) * BLK + half * TALL + i // TALL] = tiles[i]

    for m in PAIR:
        double(m, 1)
    across((2,))
    for m in PAIR:
        double(m, 2)
    for m in PAIR:
        double(m, 4)
    net.wait((2, "far"), G.at[pl.ds(0, 3), 2, 0])

    def leaf_inv(i):
        return LI[i].reshape(WIDE, WIDE)

    def coupling2(m):
        return halves([gathered(k, 2) for k in range(cols)], m)

    def mine(i):
        r, l = iota((WIDE, WIDE), 0), iota((WIDE, WIDE), 1)
        own = CORES * x + r // LANES
        return jnp.where(((r // quarter) % TALL == i) & (l // HALF == own % cols) & (r % BLK == l % BLK)
                         & ((l % HALF) // BLK == 2 * ((r // BLK) % TALL) + own // cols), 1.0, 0.0)

    def put_w(ref, val):
        ref[...] = val.reshape(TALL, TALL, 2, BLK, LANES)
        return val

    def put_z(i, val):
        ZM[i] = val[:LANES]
        ZS[i] = val[LANES:]
        net.start(ZS.at[i], ZM.at[i], partner, "z", "z")
        return val

    def t_piece(side, step, k=None):
        xx = xs(step)
        return TG.at[side, xx // 2, pl.ds(2 * (xx % 2), 2) if k is None else 2 * (xx % 2) + k]

    def t_start(side, step, k, device, name, kind="t"):
        net.start(t_piece(side, step, k), t_piece(side, step, k), device, kind, (side, name))

    def t_send(side, val):
        t_piece(side, 0)[...] = val.reshape(CORES, TALL, TALL, BLK, LANES)
        for i in PAIR:
            for s in SIDES:
                k = i if s < 0 else 1 - i
                t_start(side, 0, k, along("x", -s), (s, i))
        t_start(side, 0, None, partner, "partner", "tpair")

    def t_near(side):
        for i in PAIR:
            for s in SIDES:
                k = i if s < 0 else 1 - i
                net.wait((side, (s, i)), t_piece(side, s, k))
                if i == 0:
                    t_start(side, s, k, along("x", -s), "far")
                t_start(side, s, k, partner, "partner", "tpair")

    def t_far(side):
        net.wait((side, "far"), t_piece(side, 2))
        t_start(side, 2, None, partner, "partner", "tpair")

    def c0_pair(n):
        return [jnp.concatenate([C0[k, c, :, LANES * n:LANES * (n + 1)] for k in range(CORES)], axis=0) for c in range(cols)]

    def own_columns(first, second):
        low = iota((first.shape[0], LANES), 1) < HALF
        out = []
        for val in (first, second):
            tile = jnp.where(y // 2 == 0, val[:, :LANES], val[:, LANES:])
            moved = pltpu.roll(tile, HALF, 1)
            out.append(jnp.where(y % 2 == 0, tile, moved) if val is first else jnp.where(y % 2 == 0, moved, tile))
        return jnp.where(low, out[0], out[1])

    def w_rows(ref):
        own = CORES * x
        return ref.at[..., own % cols, :, :, own // cols, :, :]

    low_half = iota((WIDE, LANES), 1) < HALF
    blank = jnp.zeros((WIDE, WIDE), F32)

    def two_columns(one, two, coupling):
        head = own_columns(one, blank)
        return head, jnp.where(low_half, -dot(two, dot(coupling, head)), own_columns(blank, two))

    @pl.when(first_half)
    def _():
        head, tail = two_columns(leaf_inv(0), leaf_inv(1), coupling2(0))
        put_w(WL.at[0, :, 0], head)
        put_w(WL.at[0, :, 1], tail)

    @pl.when(core == 0)
    def _():
        z3 = put_z(3, dot(mine(3), leaf_inv(3)))
        put_z(2, dot(mine(2) - dot(z3, coupling2(1)), leaf_inv(2)))

    net.wait("c1", G.at[pl.ds(0, 3), 0, 0])

    def x_piece(step):
        xx = xs(step)
        return SX.at[xx // 2, pl.ds(2 * (xx % 2), 2)]

    @pl.when(first_half)
    def _():
        def own_rows(k):
            return jnp.concatenate(
                [G[k, g, x // 2, 2 * (x % 2) + kk, a] for kk in range(CORES) for g in (3, 4) for a in range(TALL)], axis=0)

        product = dot(jnp.concatenate([own_rows(k) for k in range(cols)], axis=1), WL[0].reshape(2 * WIDE, LANES))
        x_piece(0)[...] = product.reshape(CORES, 2, TALL, BLK, LANES)
        for d in range(1, chips):
            net.start(x_piece(0), x_piece(0), along("x", d), "share", "share")

    @pl.when(core == 0)
    def _():
        lhs = [jnp.concatenate([ZM[i, HALF:], ZS[i, HALF:]], axis=0) for i in (2, 3)]
        YX[y] = sum(dot(lhs[i], gathered(y, 3 + i)) for i in PAIR)
        for d in range(1, cols):
            net.start(YX.at[y], YX.at[y], along("y", d), "share", "share")


    @pl.when(first_half)
    def _():
        net.wait("c0pair", C0.at[0, 0])
        net.wait("c0far", C0.at[0, pl.ds(0, 2)])
        TP[...] = dot(jnp.concatenate(c0_pair(0), axis=1), WL[0].reshape(2 * WIDE, LANES))


    @pl.when(first_half)
    def _():
        right = c0_pair(1)
        v3 = dot(halves(right, 1), leaf_inv(3))
        v2 = dot(halves(right, 0) - dot(v3, coupling2(1)), leaf_inv(2))
        VV[:, :WIDE] = v2
        VV[:, WIDE:] = v3
        t_send(1, own_columns(v2, v3))

    net.wait("share", G.at[pl.ds(0, 3), 0, 0])

    @pl.when(first_half)
    def _():
        for g in PAIR:
            for c in range(TALL):
                for i in range(BLK):
                    SS[(g * TALL + c) * BLK + i] = SX[i % 2, c, g, i // 2]
        shared = SS[...].reshape(2 * WIDE, LANES)
        t_send(0, TP[...] - dot(VV[...], shared))
        t_near(1)
        w2 = put_w(WL.at[1, :, 0], -dot(leaf_inv(2), shared[:WIDE]))
        put_w(WL.at[1, :, 1], -dot(leaf_inv(3), shared[WIDE:] + dot(coupling2(1), w2)))
        head, tail = two_columns(leaf_inv(2), leaf_inv(3), coupling2(1))
        put_w(WR.at[:, 0], head)
        put_w(WR.at[:, 1], tail)
        net.start(w_rows(WL), w_rows(WL), partner, "w", "w")
        net.start(w_rows(WR), w_rows(WR), partner, "w", "w")
        t_near(0)

    @pl.when(core == 0)
    def _():
        none = jnp.zeros((HALF, LANES), F32)
        tiles = [jnp.concatenate([none, YX[k, :HALF], none, YX[k, HALF:]], axis=0) for k in range(cols)]
        z1 = put_z(1, dot(mine(1) - halves(tiles, 1), leaf_inv(1)))
        put_z(0, dot(mine(0) - halves(tiles, 0) - dot(z1, coupling2(0)), leaf_inv(0)))
        net.wait("w", G.at[0, pl.ds(0, 3), 0, pl.ds(0, 2)])


    @pl.when(first_half)
    def _():
        net.wait("z", ZM)

    o_ref[upper, far] = jnp.zeros((LANES, WIDE), F32)
    for i in range(TALL):
        lines = slice(quarter * i, quarter * (i + 1))
        o_ref[lines, :LANES] = WL[i // 2, spot, i % 2, :, hh].reshape(quarter, LANES)
        o_ref[lines, LANES:WIDE] = WR[spot, i % 2, :, hh].reshape(quarter, LANES) if i >= 2 else jnp.zeros((quarter, LANES), F32)
    o_ref[lower, far] = jnp.concatenate([own_columns(ZM[2 * n], ZM[2 * n + 1]) for n in PAIR], axis=1)

    def x21(side):
        total = 0.0
        for i in range(TALL):
            part = jnp.concatenate([TG[side, b % 2, c, i, b // 2] for c in range(TALL) for b in range(BLK)], axis=0)
            total = total - dot(ZM[i], part)
        o_ref[lower, LANES * side:LANES * (side + 1)] = total

    for side in (1, 0):

        @pl.when(first_half)
        def _():
            t_far(side)

        @pl.when(core == 0)
        def _():
            net.wait((side, "partner"), TG.at[side])

        x21(side)

    for name in ("leaf", 0, 1, 2):
        net.wait(name, G.at[0, :, 0], "send")
    net.wait("link", U, "send")
    net.wait("rest", G.at[pl.ds(0, 3), 0, 0], "send")
    net.wait("share", G.at[pl.ds(0, 3), 0, 0], "send")
    net.wait("pair", U.at[0], "send")
    net.wait("c0", C0.at[0, pl.ds(0, 2)], "send")

    @pl.when(first_half)
    def _():
        net.wait("c0far", C0.at[0, pl.ds(0, 2)], "send")
        net.wait("t", G.at[:, pl.ds(0, 3), 0], "send")
        net.wait("tpair", TG, "send")
        net.wait("w", G.at[0, pl.ds(0, 3), 0, pl.ds(0, 2)], "send")

    @pl.when(core == 0)
    def _():
        net.wait("c0pair", C0.at[0, 0], "send")
        net.wait("z", ZM, "send")

    counts = [len([key for key in net.names if key[0] == side]) for side in ("send", "recv")]
    assert counts == [send.shape[0], recv.shape[0]], counts


def solution(mesh):
    rows, cols = mesh.shape["row"], mesh.shape["col"]
    block_spec = P(("batch", "row"), "col")

    def device_body(local_l):
        vmem = functools.partial(pltpu.VMEM, dtype=F32)
        return pl.pallas_call(
            functools.partial(kernel, rows, cols),
            out_shape=pltpu.VMEM(local_l.shape, F32),
            in_specs=[pl.BlockSpec(memory_space=pl.ANY)],
            out_specs=pl.BlockSpec(memory_space=pltpu.VMEM),
            scratch_shapes=[
                vmem(local_l.shape),
                vmem((2, GROUPS, TALL, BLK, LANES)),
                vmem((cols, GROUPS, 2, TALL, TALL, BLK, LANES)),
                vmem((CORES, cols, LANES, WIDE)),
                vmem((TALL, TALL * BLK, BLK, WIDE)),
                vmem((TALL, 2 * BLK, BLK, WIDE)),
                vmem((TALL, TALL * BLK, BLK, WIDE)),
                vmem((2, cols, 2, TALL, 2, BLK, LANES)),
                vmem((cols, 2, TALL, 2, BLK, LANES)),
                vmem((TALL, LANES, WIDE)),
                vmem((TALL, LANES, WIDE)),
                vmem((2, 2, TALL, TALL, TALL, BLK, LANES)),
                vmem((2, TALL, 2, TALL, BLK, LANES)),
                vmem((cols, LANES, LANES)),
                vmem((WIDE, 2 * WIDE)),
                vmem((2 * TALL * BLK, BLK, LANES)),
                vmem((WIDE, LANES)),
                pltpu.SemaphoreType.DMA((3,)),
                pltpu.SemaphoreType.DMA((15,)),
                pltpu.SemaphoreType.DMA((45,)),
            ],
            compiler_params=pltpu.CompilerParams(collective_id=0, has_side_effects=True),
        )(local_l)

    return jax.shard_map(device_body, mesh=mesh, in_specs=(block_spec,), out_specs=block_spec, check_vma=False)
```

profile of v0, /device:TPU:97, one launch (start us, length us, event | category | flops | bytes accessed | tf_op | source)
XLA Modules:
  0.0 39.1 jit_solution(2355125684642514992)
XLA Ops:
  0.0 38.3 %shard_map.17 = f32[256,512]{1,0:T(8,128)S(1)} custom-call(f32[256,512]{1,0:T(8,128)} %hbm_ref.1), custom_call_target="tpu_custom_call" | custom-call | tf_op jit(solution)/shard_map/pallas_call | solution.py:506
  38.3 0.8 %copy.3 = f32[256,512]{1,0:T(8,128)} copy(f32[256,512]{1,0:T(8,128)S(1)} %shard_map.17) | data formatting | bytes 1048576
where the time goes:
time: 39.2 us; the launch traced here: 39.1 us
  Pallas kernels  38.3 us (98%)
  local copies, waits for them, and re-layouts  0.8 us (2%)
    pallas_call x1, Pallas kernels, device_body(): pl.pallas_call(functools.partial(kernel, rows, cols), out_shape=pltpu.VME...  38.3 us
    unnamed x1, local copies, waits for them, and re-layouts  0.8 us

commit v1 on v0

--- a/solution.py
+++ b/solution.py
@@ -120,7 +120,7 @@
     C0[core, y] = l_ref[lower, near]
     pl.semaphore_wait(barrier, len(peers))
 
-    axis_first = ["x", "y", "y"]
+    axis_first = ["y", "y", "x"]
 
     def other(axis):
         return "y" if axis == "x" else "x"

time: 39.2 us -> 43 us (1.097)
  Pallas kernels: 38.3 us -> 42.1 us
    pallas_call x1, Pallas kernels: 38.3 us -> 42.1 us  [device_body(): pl.pallas_call(functools.partial(kernel, rows, cols), out_shape=pltpu.VME...]
where the time goes in v1:
time: 43 us; the launch traced here: 42.9 us
  Pallas kernels  42.1 us (98%)
  local copies, waits for them, and re-layouts  0.8 us (2%)
    pallas_call x1, Pallas kernels, device_body(): pl.pallas_call(functools.partial(kernel, rows, cols), out_shape=pltpu.VME...  42.1 us

profile of v1, /device:TPU:97, one launch (start us, length us, event | category | flops | bytes accessed | tf_op | source)
XLA Modules:
  0.0 42.9 jit_solution(11014788530457608523)
XLA Ops:
  0.0 42.1 %shard_map.17 = f32[256,512]{1,0:T(8,128)S(1)} custom-call(f32[256,512]{1,0:T(8,128)} %hbm_ref.1), custom_call_target="tpu_custom_call" | custom-call | tf_op jit(solution)/shard_map/pallas_call | solution.py:506
  42.1 0.8 %copy.3 = f32[256,512]{1,0:T(8,128)} copy(f32[256,512]{1,0:T(8,128)S(1)} %shard_map.17) | data formatting | bytes 1048576
